TPU v7x, 32 devices: a whole 2x2x4 slice. The times are simulated.
32 devices in a mesh: groups: 2 (over y), dom: 8 (over z, core), tilt: 2 (over x), rep: 1.
Axes of the slice: x: 2, y: 2, z: 4, core: 2. Of those that a mesh axis runs over, the one named last changes fastest.
Arguments:
- patches: bfloat16 [4, 1024, 128, 128], P(('groups', 'tilt'), 'dom'), parts along dimension 0, may hold values from -6 to 6
- slot_view: int32 [4, 1024, 1], P(('groups', 'tilt'), 'dom'), parts along dimension 0, may hold values from 0 to 31, as said below
- slot_tilt: int32 [4, 1024], P(('groups', 'tilt'), 'dom'), parts along dimension 0, may hold values from 0 to 9
- slot_pos: bfloat16 [2, 4, 1024], P(None, ('groups', 'tilt'), 'dom'), parts along dimension 1, may hold values from 0 to 1
- defocus: bfloat16 [4, 1024], P(('groups', 'tilt'), 'dom'), parts along dimension 0, may hold values from 1 to 3
- projections: bfloat16 [64, 20, 2, 128, 128], P(('groups', 'dom'), 'tilt', None, 'rep'), parts along dimension 0, may hold values from -6 to 6
- warp_grid: float32 [40, 2, 256], P(('groups', 'tilt')), parts along dimension 0, may hold values from -6 to 6
Outputs:
- slot_terms: float32 [3, 4, 1024], P(None, ('groups', 'tilt'), 'dom'), parts along dimension 1
- new_warp: float32 [40, 2, 256], P(('groups', 'tilt')), parts along dimension 0
There are 2 independent parts, one for each index of `groups`. A program takes and returns all parts, laid end to end along the dimension named above; each array names one. Nothing has to cross between parts.
Inputs may be any that keep to these rules, and one draw needn't show every extreme that they name: `slot_view`: view v is owned by dom index v // 4. Among the 128 slots of one device (one tilt index and one dom index) at most 24 name views of any one owner, and in every such block some owner is named exactly 24 times.
All inputs are finite; a program needn't handle non-finite values.
Results may differ from a plain program's by a relative error of at most 0.0018.
Values may be sent and summed in bfloat16 or wider, within the bound.
A program may use at most 64 MiB of HBM per device.

v0:
```python
import math
import jax
import jax.numpy as jnp
from jax import lax
from jax.sharding import PartitionSpec as P

GRID = 16
AMPLITUDE = 0.07
TRUST_FLOOR = 0.02


def signed_freq(index, pixels):
    return jnp.where(index < pixels // 2, index, index - pixels).astype(jnp.float32)


def dft_tables(freq_rows, pixels):
    columns = jnp.arange(pixels, dtype=jnp.int32)
    table_scale = 1.0 / math.sqrt(pixels)
    turns_rows = (freq_rows[:, None] * columns[None, :] % pixels).astype(jnp.float32) * (
        2.0 * math.pi / pixels
    )
    turns_full = (columns[:, None] * columns[None, :] % pixels).astype(jnp.float32) * (
        2.0 * math.pi / pixels
    )
    row_table = jnp.concatenate([jnp.cos(turns_rows), jnp.sin(turns_rows)], axis=0) * table_scale
    col_table = jnp.concatenate([jnp.cos(turns_full), jnp.sin(turns_full)], axis=1) * table_scale
    return (row_table.astype(jnp.bfloat16), col_table.astype(jnp.bfloat16))


def node_weights(pos_x, pos_y, grid_side):
    knot_pos = jnp.arange(grid_side, dtype=jnp.int32).astype(jnp.float32)
    weight_x = jnp.maximum(0.0, 1.0 - jnp.abs(pos_x[:, None] * (grid_side - 1) - knot_pos[None, :]))
    weight_y = jnp.maximum(0.0, 1.0 - jnp.abs(pos_y[:, None] * (grid_side - 1) - knot_pos[None, :]))
    return (weight_y[:, :, None] * weight_x[:, None, :]).reshape(
        pos_x.shape[0], grid_side * grid_side
    )


def spectral_terms(spectrum, ref_blk, focus_blk, shift_blk, freq_rows, pixels):
    row_total = freq_rows.shape[0]
    v_one_cos = spectrum[:, :row_total, :pixels]
    v_one_sin = spectrum[:, :row_total, pixels:]
    v_two_cos = spectrum[:, row_total:, :pixels]
    v_two_sin = spectrum[:, row_total:, pixels:]
    real_part = v_one_cos - v_two_sin
    imag_part = -(v_one_sin + v_two_cos)
    freq_y = signed_freq(freq_rows, pixels)[None, :, None]
    freq_x = signed_freq(jnp.arange(pixels, dtype=jnp.int32), pixels)[None, None, :]
    nyquist = pixels / 2.0
    radius = (freq_y * freq_y + freq_x * freq_x) / (nyquist * nyquist)
    aberration = math.pi * focus_blk[:, None, None] * radius
    contrast = -(
        math.sqrt(1.0 - AMPLITUDE * AMPLITUDE) * jnp.sin(aberration)
        + AMPLITUDE * jnp.cos(aberration)
    )
    phase_angle = (
        2.0
        * math.pi
        / pixels
        * (freq_x * shift_blk[:, 0, None, None] + freq_y * shift_blk[:, 1, None, None])
    )
    cosine = jnp.cos(phase_angle)
    sine_part = jnp.sin(phase_angle)
    ref_real = ref_blk[:, 0].astype(jnp.float32)
    ref_imag = ref_blk[:, 1].astype(jnp.float32)
    model_real = contrast * (ref_real * cosine + ref_imag * sine_part)
    model_imag = contrast * (ref_imag * cosine - ref_real * sine_part)
    diff_real = real_part - model_real
    diff_imag = imag_part - model_imag
    inverse_area = 1.0 / (pixels * pixels)
    energy = jnp.sum(diff_real * diff_real + diff_imag * diff_imag, axis=(1, 2)) * inverse_area
    cross_term = diff_imag * model_real - diff_real * model_imag
    grad_x = 2.0 * inverse_area * jnp.sum(2.0 * math.pi / pixels * freq_x * cross_term, axis=(1, 2))
    grad_y = 2.0 * inverse_area * jnp.sum(2.0 * math.pi / pixels * freq_y * cross_term, axis=(1, 2))
    return jnp.stack([energy, grad_x, grad_y], axis=1)


def on_device(patches, slot_view, slot_tilt, slot_pos, defocus, projections, warp_grid):
    owners = lax.axis_size("dom")
    slot_count = patches.shape[1]
    pixels = patches.shape[-1]
    view_dev = projections.shape[0]
    tilt_dev = warp_grid.shape[0]
    node_count = warp_grid.shape[2]
    capacity = 3 * slot_count // (2 * owners)
    buffer_len = owners * capacity
    chosen_view = slot_view[0, :, 0]
    owner_of = chosen_view // view_dev
    owner_hits = (owner_of[:, None] == jnp.arange(owners, dtype=jnp.int32)[None, :]).astype(
        jnp.int32
    )
    earlier = jnp.cumsum(owner_hits, axis=0) - owner_hits
    slot_rank = jnp.sum(earlier * owner_hits, axis=1)
    target = owner_of * capacity + slot_rank
    matches = target[None, :] == jnp.arange(buffer_len, dtype=jnp.int32)[:, None]
    source = jnp.sum(
        jnp.where(matches, jnp.arange(slot_count, dtype=jnp.int32)[None, :], 0), axis=1
    )
    filled = jnp.any(matches, axis=1)
    patch_rows = jnp.where(filled[:, None, None], patches[0][source], jnp.zeros((), jnp.bfloat16))
    slot_meta = jnp.stack(
        [
            slot_tilt[0].astype(jnp.float32),
            (chosen_view % view_dev).astype(jnp.float32),
            defocus[0].astype(jnp.float32),
            slot_pos[0, 0].astype(jnp.float32),
            slot_pos[1, 0].astype(jnp.float32),
            jnp.ones((slot_count,), jnp.float32),
        ],
        axis=1,
    )
    meta_rows = jnp.where(filled[:, None], slot_meta[source], 0.0).astype(jnp.bfloat16)
    patch_buffer = patch_rows.reshape(owners, capacity, pixels, pixels)
    meta_buffer = meta_rows.reshape(owners, capacity, 6)
    row_span = projections.shape[3]
    freq_rows = lax.axis_index("rep") * row_span + jnp.arange(row_span, dtype=jnp.int32)
    row_table, col_table = dft_tables(freq_rows, pixels)
    row_total = freq_rows.shape[0]
    projected_flat = projections.reshape(view_dev * tilt_dev, 2, row_total, pixels)
    tilt_iota = jnp.arange(tilt_dev, dtype=jnp.int32)
    view_iota = jnp.arange(view_dev, dtype=jnp.int32)

    def one_block(inputs):
        patch_blk, index_blk, focus_blk, shift_blk = inputs
        ref_blk = projected_flat[index_blk]
        first_pass = jnp.einsum(
            "fy,byx->bfx", row_table, patch_blk, preferred_element_type=jnp.float32
        ).astype(jnp.bfloat16)
        spectrum = jnp.einsum(
            "bfx,xk->bfk", first_pass, col_table, preferred_element_type=jnp.float32
        )
        return spectral_terms(spectrum, ref_blk, focus_blk, shift_blk, freq_rows, pixels)

    patch_in = lax.all_to_all(patch_buffer, "dom", split_axis=0, concat_axis=0, tiled=True)
    meta_in = lax.all_to_all(meta_buffer, "dom", split_axis=0, concat_axis=0, tiled=True)
    senders = patch_in.shape[0]
    per_sender = patch_in.shape[1]
    slot_total = senders * per_sender
    meta_flat = meta_in.reshape(slot_total, 6).astype(jnp.float32)
    tilt_match = meta_flat[:, 0:1] == tilt_iota.astype(jnp.float32)[None, :]
    view_match = meta_flat[:, 1:2] == view_iota.astype(jnp.float32)[None, :]
    tilt_local = jnp.sum(jnp.where(tilt_match, tilt_iota[None, :], 0), axis=1)
    view_local = jnp.sum(jnp.where(view_match, view_iota[None, :], 0), axis=1)
    weights = node_weights(meta_flat[:, 3], meta_flat[:, 4], GRID)
    shifts = jnp.sum(warp_grid[tilt_local] * weights[:, None, :], axis=2)
    block_len = math.gcd(slot_total, 16)
    block_count = slot_total // block_len
    per_slot = lax.map(
        one_block,
        (
            patch_in.reshape(block_count, block_len, pixels, pixels),
            (view_local * tilt_dev + tilt_local).reshape(block_count, block_len),
            meta_flat[:, 2].reshape(block_count, block_len),
            shifts.reshape(block_count, block_len, 2),
        ),
    ).reshape(slot_total, 3)
    node_coef = (
        tilt_match.astype(jnp.float32)[:, :, None]
        * per_slot[:, None, 1:3]
        * meta_flat[:, 5, None, None]
    ).reshape(senders, per_sender, 2 * tilt_dev)
    returned = lax.all_to_all(
        per_slot.reshape(senders, per_sender, 3), "dom", split_axis=0, concat_axis=0, tiled=True
    )
    weight_all = weights.reshape(senders, per_sender, node_count)
    own_terms = returned.reshape(buffer_len, 3)[target]
    summed = lax.psum(own_terms, "rep")
    slot_terms = summed.T[:, None, :]
    gradient = jnp.dot(
        node_coef.reshape(-1, 2 * tilt_dev).T,
        weight_all.reshape(-1, node_count),
        precision=lax.Precision.HIGHEST,
        preferred_element_type=jnp.float32,
    ).reshape(tilt_dev, 2, node_count)
    whole_grad = lax.psum(gradient, ("dom", "rep"))
    new_warp = warp_grid - whole_grad / jnp.sqrt(
        whole_grad * whole_grad + TRUST_FLOOR * TRUST_FLOOR
    )
    return (slot_terms, new_warp)


def solution(mesh):
    in_specs = (
        P(("groups", "tilt"), "dom", None, None),
        P(("groups", "tilt"), "dom", None),
        P(("groups", "tilt"), "dom"),
        P(None, ("groups", "tilt"), "dom"),
        P(("groups", "tilt"), "dom"),
        P(("groups", "dom"), "tilt", None, "rep", None),
        P(("groups", "tilt"), None, None),
    )
    out_specs = (P(None, ("groups", "tilt"), "dom"), P(("groups", "tilt"), None, None))
    return jax.shard_map(
        on_device, mesh=mesh, in_specs=in_specs, out_specs=out_specs, check_vma=False
    )
```

profile of v0, /device:TPU:0, one launch (start us, length us, event | category | flops | bytes accessed | tf_op | source)
XLA Modules:
  0.0 444.6 jit_solution(1007006649997248516)
XLA Ops:
  0.6 0.7 and_select_fusion.2
  1.7 0.7 fusion.48
  2.4 0.7 multiply_add_fusion.1
  3.3 0.7 bitcast_convert_fusion
  4.1 0.7 convert_bitcast_fusion
  4.7 0.7 stack.8
  5.6 0.8 gather_fusion.2
  6.5 0.6 select_convert_fusion
  7.2 6.4 %all-to-all-start.1 = ((bf16[8,24,6]{1,2,0:T(8,128)(2,1)}), bf16[8,24,6]{1,2,0:T(8,128)(2,1)S(1)}, u32[]{:S(2)}, u32[]{:S(2)}) async-start(bf16[8,24,6]{1,2,0:T(8,128)(2,1)} %select_convert_fusion), calls=%async_computation.1 | async-start | bytes 32768 | tf_op jit(solution)/shard_map/all_to_all | solution.py:135
  13.5 10.2 %gather_fusion.1 = bf16[192,128,128]{2,1,0:T(8,128)(2,1)} fusion(bf16[128,128,128]{2,1,0:T(8,128)(2,1)} %bitcast.181, s32[1024]{0:T(1024)S(1)} %pad_clamp_fusion.3), kind=kCustom, calls=%fused_computation.1 | custom fusion | bytes 12583680 | tf_op jit(solution)/shard_map/gather | solution.py:100
  23.8 8.6 %copy.103 = bf16[8,24,128,128]{2,3,1,0:T(8,128)(2,1)} copy(bf16[8,24,128,128]{3,2,1,0:T(8,128)(2,1)} %bitcast.179) | data formatting | bytes 12582912 | tf_op jit(solution)/shard_map/gather | solution.py:100
  32.4 5.9 %broadcast_select_fusion = bf16[8,24,128,128]{2,3,1,0:T(8,128)(2,1)} fusion(bf16[8,24,128,128]{2,3,1,0:T(8,128)(2,1)} %copy.103, pred[8,24]{1,0:T(8,128)(4,1)S(1)} %broadcast_in_dim.106), kind=kLoop, calls=%fused_computation.65 | loop fusion | flops 3145728 | bytes 12583104 | tf_op jit(solution)/shard_map/jit(_where)/select_n | solution.py:100
  38.3 5.2 %all-to-all-start = ((bf16[8,24,128,128]{2,3,1,0:T(8,128)(2,1)}), bf16[8,24,128,128]{2,3,1,0:T(8,128)(2,1)}, u32[]{:S(2)}, u32[]{:S(2)}) async-start(bf16[8,24,128,128]{2,3,1,0:T(8,128)(2,1)} %broadcast_select_fusion), calls=%async_computation | async-start | bytes 12582912 | tf_op jit(solution)/shard_map/all_to_all | solution.py:134
  44.4 1.1 gather_fusion.3
  46.3 136.3 %all-to-all-done = bf16[8,24,128,128]{2,3,1,0:T(8,128)(2,1)} async-done(((bf16[8,24,128,128]{2,3,1,0:T(8,128)(2,1)}), bf16[8,24,128,128]{2,3,1,0:T(8,128)(2,1)}, u32[]{:S(2)}, u32[]{:S(2)}) %all-to-all-start) | async-done | bytes 6291488 | tf_op jit(solution)/shard_map/all_to_all | solution.py:134
  182.6 223.7 %while.15 = (s32[]{:T(128)}, f32[12,16,3]{1,0,2:T(8,128)S(1)}, bf16[12,16,128,128]{2,3,1,0:T(8,128)(2,1)}, bf16[256,128]{1,0:T(8,128)(2,1)S(1)}, bf16[128,256]{1...) while((s32[]{:T(128)}, f32[12,16,3]{1,0,2:T(8,128)S(1)}, ...), condition=%wide.region_11.12_spmd.clone.clone, body=%wide.region_7.11_spmd.clone.clone.sunk | while | flops 411868064 | bytes 14461309 | solution.py:148
  182.7 4.5 %fusion.62 = f32[16,256,256]{2,1,0:T(8,128)} fusion(bf16[12,16,128,128]{2,3,1,0:T(8,128)(2,1)} %get-tuple-element.403, s32[]{:T(128)} %get-tuple-element.390, bf16[128,256]{1,0:T(8,128)(2,1)S(1)} %get-tuple-element.405, bf16[256,128]{1,0:T(8,128)(2,1)S(1)} %get-tuple-element.404), kind=kOutput, calls=%fused_computation.10.clone.1 | convolution fusion | flops 403177472 | bytes 4850176 | tf_op jit(solution)/shard_map/while/body/eval_jaxpr/bfx,xk->bfk/dot_general | solution.py:129
  187.2 2.5 gather_fusion
  189.8 10.9 %add_reduce_fusion.2 = (f32[16]{0:T(128)S(1)}, f32[16,128,128]{2,1,0:T(8,128)S(1)}) fusion(f32[16,256,256]{2,1,0:T(8,128)} %fusion.62, bf16[16,2,128,128]{3,2,1,0:T(8,128)(2,1)S(1)} %gather_fusion, f32[16,128]{1,0:T(8,128)S(1)} %get-tuple-element.371, f32[16,128]{1,0:T(8,128)S(1)} %get-tuple-element.372, f32[128,128]{1,0:T(8,128)S(1)} %add_multiply_fusion.3, ...), kind=kLoop, calls=%fused_computation.31.clone.1 | loop fusion | flops 7602160 | bytes 6373504 | tf_op jit(solution)/shard_map/while/body/eval_jaxpr/reduce_sum | solution.py:71
  200.8 0.3 multiply_reduce_fusion.4
  201.3 4.5 %fusion.62 = f32[16,256,256]{2,1,0:T(8,128)} fusion(bf16[12,16,128,128]{2,3,1,0:T(8,128)(2,1)} %get-tuple-element.403, s32[]{:T(128)} %get-tuple-element.390, bf16[128,256]{1,0:T(8,128)(2,1)S(1)} %get-tuple-element.405, bf16[256,128]{1,0:T(8,128)(2,1)S(1)} %get-tuple-element.404), kind=kOutput, calls=%fused_computation.10.clone.1 | convolution fusion | flops 403177472 | bytes 4850176 | tf_op jit(solution)/shard_map/while/body/eval_jaxpr/bfx,xk->bfk/dot_general | solution.py:129
  205.9 2.5 gather_fusion
  208.5 10.9 %add_reduce_fusion.2 = (f32[16]{0:T(128)S(1)}, f32[16,128,128]{2,1,0:T(8,128)S(1)}) fusion(f32[16,256,256]{2,1,0:T(8,128)} %fusion.62, bf16[16,2,128,128]{3,2,1,0:T(8,128)(2,1)S(1)} %gather_fusion, f32[16,128]{1,0:T(8,128)S(1)} %get-tuple-element.371, f32[16,128]{1,0:T(8,128)S(1)} %get-tuple-element.372, f32[128,128]{1,0:T(8,128)S(1)} %add_multiply_fusion.3, ...), kind=kLoop, calls=%fused_computation.31.clone.1 | loop fusion | flops 7602160 | bytes 6373504 | tf_op jit(solution)/shard_map/while/body/eval_jaxpr/reduce_sum | solution.py:71
  219.4 0.3 multiply_reduce_fusion.4
  220.0 4.5 %fusion.62 = f32[16,256,256]{2,1,0:T(8,128)} fusion(bf16[12,16,128,128]{2,3,1,0:T(8,128)(2,1)} %get-tuple-element.403, s32[]{:T(128)} %get-tuple-element.390, bf16[128,256]{1,0:T(8,128)(2,1)S(1)} %get-tuple-element.405, bf16[256,128]{1,0:T(8,128)(2,1)S(1)} %get-tuple-element.404), kind=kOutput, calls=%fused_computation.10.clone.1 | convolution fusion | flops 403177472 | bytes 4850176 | tf_op jit(solution)/shard_map/while/body/eval_jaxpr/bfx,xk->bfk/dot_general | solution.py:129
  224.5 2.5 gather_fusion
  227.1 10.9 %add_reduce_fusion.2 = (f32[16]{0:T(128)S(1)}, f32[16,128,128]{2,1,0:T(8,128)S(1)}) fusion(f32[16,256,256]{2,1,0:T(8,128)} %fusion.62, bf16[16,2,128,128]{3,2,1,0:T(8,128)(2,1)S(1)} %gather_fusion, f32[16,128]{1,0:T(8,128)S(1)} %get-tuple-element.371, f32[16,128]{1,0:T(8,128)S(1)} %get-tuple-element.372, f32[128,128]{1,0:T(8,128)S(1)} %add_multiply_fusion.3, ...), kind=kLoop, calls=%fused_computation.31.clone.1 | loop fusion | flops 7602160 | bytes 6373504 | tf_op jit(solution)/shard_map/while/body/eval_jaxpr/reduce_sum | solution.py:71
  238.1 0.3 multiply_reduce_fusion.4
  238.6 4.5 %fusion.62 = f32[16,256,256]{2,1,0:T(8,128)} fusion(bf16[12,16,128,128]{2,3,1,0:T(8,128)(2,1)} %get-tuple-element.403, s32[]{:T(128)} %get-tuple-element.390, bf16[128,256]{1,0:T(8,128)(2,1)S(1)} %get-tuple-element.405, bf16[256,128]{1,0:T(8,128)(2,1)S(1)} %get-tuple-element.404), kind=kOutput, calls=%fused_computation.10.clone.1 | convolution fusion | flops 403177472 | bytes 4850176 | tf_op jit(solution)/shard_map/while/body/eval_jaxpr/bfx,xk->bfk/dot_general | solution.py:129
  243.2 2.5 gather_fusion
  245.8 10.9 %add_reduce_fusion.2 = (f32[16]{0:T(128)S(1)}, f32[16,128,128]{2,1,0:T(8,128)S(1)}) fusion(f32[16,256,256]{2,1,0:T(8,128)} %fusion.62, bf16[16,2,128,128]{3,2,1,0:T(8,128)(2,1)S(1)} %gather_fusion, f32[16,128]{1,0:T(8,128)S(1)} %get-tuple-element.371, f32[16,128]{1,0:T(8,128)S(1)} %get-tuple-element.372, f32[128,128]{1,0:T(8,128)S(1)} %add_multiply_fusion.3, ...), kind=kLoop, calls=%fused_computation.31.clone.1 | loop fusion | flops 7602160 | bytes 6373504 | tf_op jit(solution)/shard_map/while/body/eval_jaxpr/reduce_sum | solution.py:71
  256.7 0.3 multiply_reduce_fusion.4
  257.3 4.5 %fusion.62 = f32[16,256,256]{2,1,0:T(8,128)} fusion(bf16[12,16,128,128]{2,3,1,0:T(8,128)(2,1)} %get-tuple-element.403, s32[]{:T(128)} %get-tuple-element.390, bf16[128,256]{1,0:T(8,128)(2,1)S(1)} %get-tuple-element.405, bf16[256,128]{1,0:T(8,128)(2,1)S(1)} %get-tuple-element.404), kind=kOutput, calls=%fused_computation.10.clone.1 | convolution fusion | flops 403177472 | bytes 4850176 | tf_op jit(solution)/shard_map/while/body/eval_jaxpr/bfx,xk->bfk/dot_general | solution.py:129
  261.8 2.5 gather_fusion
  264.4 10.9 %add_reduce_fusion.2 = (f32[16]{0:T(128)S(1)}, f32[16,128,128]{2,1,0:T(8,128)S(1)}) fusion(f32[16,256,256]{2,1,0:T(8,128)} %fusion.62, bf16[16,2,128,128]{3,2,1,0:T(8,128)(2,1)S(1)} %gather_fusion, f32[16,128]{1,0:T(8,128)S(1)} %get-tuple-element.371, f32[16,128]{1,0:T(8,128)S(1)} %get-tuple-element.372, f32[128,128]{1,0:T(8,128)S(1)} %add_multiply_fusion.3, ...), kind=kLoop, calls=%fused_computation.31.clone.1 | loop fusion | flops 7602160 | bytes 6373504 | tf_op jit(solution)/shard_map/while/body/eval_jaxpr/reduce_sum | solution.py:71
  275.9 4.5 %fusion.62 = f32[16,256,256]{2,1,0:T(8,128)} fusion(bf16[12,16,128,128]{2,3,1,0:T(8,128)(2,1)} %get-tuple-element.403, s32[]{:T(128)} %get-tuple-element.390, bf16[128,256]{1,0:T(8,128)(2,1)S(1)} %get-tuple-element.405, bf16[256,128]{1,0:T(8,128)(2,1)S(1)} %get-tuple-element.404), kind=kOutput, calls=%fused_computation.10.clone.1 | convolution fusion | flops 403177472 | bytes 4850176 | tf_op jit(solution)/shard_map/while/body/eval_jaxpr/bfx,xk->bfk/dot_general | solution.py:129
  280.5 2.5 gather_fusion
  283.1 10.9 %add_reduce_fusion.2 = (f32[16]{0:T(128)S(1)}, f32[16,128,128]{2,1,0:T(8,128)S(1)}) fusion(f32[16,256,256]{2,1,0:T(8,128)} %fusion.62, bf16[16,2,128,128]{3,2,1,0:T(8,128)(2,1)S(1)} %gather_fusion, f32[16,128]{1,0:T(8,128)S(1)} %get-tuple-element.371, f32[16,128]{1,0:T(8,128)S(1)} %get-tuple-element.372, f32[128,128]{1,0:T(8,128)S(1)} %add_multiply_fusion.3, ...), kind=kLoop, calls=%fused_computation.31.clone.1 | loop fusion | flops 7602160 | bytes 6373504 | tf_op jit(solution)/shard_map/while/body/eval_jaxpr/reduce_sum | solution.py:71
  294.6 4.5 %fusion.62 = f32[16,256,256]{2,1,0:T(8,128)} fusion(bf16[12,16,128,128]{2,3,1,0:T(8,128)(2,1)} %get-tuple-element.403, s32[]{:T(128)} %get-tuple-element.390, bf16[128,256]{1,0:T(8,128)(2,1)S(1)} %get-tuple-element.405, bf16[256,128]{1,0:T(8,128)(2,1)S(1)} %get-tuple-element.404), kind=kOutput, calls=%fused_computation.10.clone.1 | convolution fusion | flops 403177472 | bytes 4850176 | tf_op jit(solution)/shard_map/while/body/eval_jaxpr/bfx,xk->bfk/dot_general | solution.py:129
  299.1 2.5 gather_fusion
  301.7 10.9 %add_reduce_fusion.2 = (f32[16]{0:T(128)S(1)}, f32[16,128,128]{2,1,0:T(8,128)S(1)}) fusion(f32[16,256,256]{2,1,0:T(8,128)} %fusion.62, bf16[16,2,128,128]{3,2,1,0:T(8,128)(2,1)S(1)} %gather_fusion, f32[16,128]{1,0:T(8,128)S(1)} %get-tuple-element.371, f32[16,128]{1,0:T(8,128)S(1)} %get-tuple-element.372, f32[128,128]{1,0:T(8,128)S(1)} %add_multiply_fusion.3, ...), kind=kLoop, calls=%fused_computation.31.clone.1 | loop fusion | flops 7602160 | bytes 6373504 | tf_op jit(solution)/shard_map/while/body/eval_jaxpr/reduce_sum | solution.py:71
  313.2 4.5 %fusion.62 = f32[16,256,256]{2,1,0:T(8,128)} fusion(bf16[12,16,128,128]{2,3,1,0:T(8,128)(2,1)} %get-tuple-element.403, s32[]{:T(128)} %get-tuple-element.390, bf16[128,256]{1,0:T(8,128)(2,1)S(1)} %get-tuple-element.405, bf16[256,128]{1,0:T(8,128)(2,1)S(1)} %get-tuple-element.404), kind=kOutput, calls=%fused_computation.10.clone.1 | convolution fusion | flops 403177472 | bytes 4850176 | tf_op jit(solution)/shard_map/while/body/eval_jaxpr/bfx,xk->bfk/dot_general | solution.py:129
  317.8 2.5 gather_fusion
  320.4 10.9 %add_reduce_fusion.2 = (f32[16]{0:T(128)S(1)}, f32[16,128,128]{2,1,0:T(8,128)S(1)}) fusion(f32[16,256,256]{2,1,0:T(8,128)} %fusion.62, bf16[16,2,128,128]{3,2,1,0:T(8,128)(2,1)S(1)} %gather_fusion, f32[16,128]{1,0:T(8,128)S(1)} %get-tuple-element.371, f32[16,128]{1,0:T(8,128)S(1)} %get-tuple-element.372, f32[128,128]{1,0:T(8,128)S(1)} %add_multiply_fusion.3, ...), kind=kLoop, calls=%fused_computation.31.clone.1 | loop fusion | flops 7602160 | bytes 6373504 | tf_op jit(solution)/shard_map/while/body/eval_jaxpr/reduce_sum | solution.py:71
  331.9 4.5 %fusion.62 = f32[16,256,256]{2,1,0:T(8,128)} fusion(bf16[12,16,128,128]{2,3,1,0:T(8,128)(2,1)} %get-tuple-element.403, s32[]{:T(128)} %get-tuple-element.390, bf16[128,256]{1,0:T(8,128)(2,1)S(1)} %get-tuple-element.405, bf16[256,128]{1,0:T(8,128)(2,1)S(1)} %get-tuple-element.404), kind=kOutput, calls=%fused_computation.10.clone.1 | convolution fusion | flops 403177472 | bytes 4850176 | tf_op jit(solution)/shard_map/while/body/eval_jaxpr/bfx,xk->bfk/dot_general | solution.py:129
  336.4 2.5 gather_fusion
  339.0 10.9 %add_reduce_fusion.2 = (f32[16]{0:T(128)S(1)}, f32[16,128,128]{2,1,0:T(8,128)S(1)}) fusion(f32[16,256,256]{2,1,0:T(8,128)} %fusion.62, bf16[16,2,128,128]{3,2,1,0:T(8,128)(2,1)S(1)} %gather_fusion, f32[16,128]{1,0:T(8,128)S(1)} %get-tuple-element.371, f32[16,128]{1,0:T(8,128)S(1)} %get-tuple-element.372, f32[128,128]{1,0:T(8,128)S(1)} %add_multiply_fusion.3, ...), kind=kLoop, calls=%fused_computation.31.clone.1 | loop fusion | flops 7602160 | bytes 6373504 | tf_op jit(solution)/shard_map/while/body/eval_jaxpr/reduce_sum | solution.py:71
  350.5 4.5 %fusion.62 = f32[16,256,256]{2,1,0:T(8,128)} fusion(bf16[12,16,128,128]{2,3,1,0:T(8,128)(2,1)} %get-tuple-element.403, s32[]{:T(128)} %get-tuple-element.390, bf16[128,256]{1,0:T(8,128)(2,1)S(1)} %get-tuple-element.405, bf16[256,128]{1,0:T(8,128)(2,1)S(1)} %get-tuple-element.404), kind=kOutput, calls=%fused_computation.10.clone.1 | convolution fusion | flops 403177472 | bytes 4850176 | tf_op jit(solution)/shard_map/while/body/eval_jaxpr/bfx,xk->bfk/dot_general | solution.py:129
  355.1 2.5 gather_fusion
  357.7 10.9 %add_reduce_fusion.2 = (f32[16]{0:T(128)S(1)}, f32[16,128,128]{2,1,0:T(8,128)S(1)}) fusion(f32[16,256,256]{2,1,0:T(8,128)} %fusion.62, bf16[16,2,128,128]{3,2,1,0:T(8,128)(2,1)S(1)} %gather_fusion, f32[16,128]{1,0:T(8,128)S(1)} %get-tuple-element.371, f32[16,128]{1,0:T(8,128)S(1)} %get-tuple-element.372, f32[128,128]{1,0:T(8,128)S(1)} %add_multiply_fusion.3, ...), kind=kLoop, calls=%fused_computation.31.clone.1 | loop fusion | flops 7602160 | bytes 6373504 | tf_op jit(solution)/shard_map/while/body/eval_jaxpr/reduce_sum | solution.py:71
  369.2 4.5 %fusion.62 = f32[16,256,256]{2,1,0:T(8,128)} fusion(bf16[12,16,128,128]{2,3,1,0:T(8,128)(2,1)} %get-tuple-element.403, s32[]{:T(128)} %get-tuple-element.390, bf16[128,256]{1,0:T(8,128)(2,1)S(1)} %get-tuple-element.405, bf16[256,128]{1,0:T(8,128)(2,1)S(1)} %get-tuple-element.404), kind=kOutput, calls=%fused_computation.10.clone.1 | convolution fusion | flops 403177472 | bytes 4850176 | tf_op jit(solution)/shard_map/while/body/eval_jaxpr/bfx,xk->bfk/dot_general | solution.py:129
  373.7 2.5 gather_fusion
  376.3 10.9 %add_reduce_fusion.2 = (f32[16]{0:T(128)S(1)}, f32[16,128,128]{2,1,0:T(8,128)S(1)}) fusion(f32[16,256,256]{2,1,0:T(8,128)} %fusion.62, bf16[16,2,128,128]{3,2,1,0:T(8,128)(2,1)S(1)} %gather_fusion, f32[16,128]{1,0:T(8,128)S(1)} %get-tuple-element.371, f32[16,128]{1,0:T(8,128)S(1)} %get-tuple-element.372, f32[128,128]{1,0:T(8,128)S(1)} %add_multiply_fusion.3, ...), kind=kLoop, calls=%fused_computation.31.clone.1 | loop fusion | flops 7602160 | bytes 6373504 | tf_op jit(solution)/shard_map/while/body/eval_jaxpr/reduce_sum | solution.py:71
  387.8 4.5 %fusion.62 = f32[16,256,256]{2,1,0:T(8,128)} fusion(bf16[12,16,128,128]{2,3,1,0:T(8,128)(2,1)} %get-tuple-element.403, s32[]{:T(128)} %get-tuple-element.390, bf16[128,256]{1,0:T(8,128)(2,1)S(1)} %get-tuple-element.405, bf16[256,128]{1,0:T(8,128)(2,1)S(1)} %get-tuple-element.404), kind=kOutput, calls=%fused_computation.10.clone.1 | convolution fusion | flops 403177472 | bytes 4850176 | tf_op jit(solution)/shard_map/while/body/eval_jaxpr/bfx,xk->bfk/dot_general | solution.py:129
  392.4 2.5 gather_fusion
  395.0 10.9 %add_reduce_fusion.2 = (f32[16]{0:T(128)S(1)}, f32[16,128,128]{2,1,0:T(8,128)S(1)}) fusion(f32[16,256,256]{2,1,0:T(8,128)} %fusion.62, bf16[16,2,128,128]{3,2,1,0:T(8,128)(2,1)S(1)} %gather_fusion, f32[16,128]{1,0:T(8,128)S(1)} %get-tuple-element.371, f32[16,128]{1,0:T(8,128)S(1)} %get-tuple-element.372, f32[128,128]{1,0:T(8,128)S(1)} %add_multiply_fusion.3, ...), kind=kLoop, calls=%fused_computation.31.clone.1 | loop fusion | flops 7602160 | bytes 6373504 | tf_op jit(solution)/shard_map/while/body/eval_jaxpr/reduce_sum | solution.py:71
  406.6 0.3 fusion.42
  406.9 26.7 %psum.6 = f32[10,2,256]{2,0,1:T(8,128)S(1)} all-reduce(f32[10,2,256]{2,0,1:T(8,128)S(1)} %fusion.42), channel_id=1, replica_groups=mesh['groups'=2,'dom'=8,'tilt'=2,'rep'=1] {'dom','rep'}, use_global_device_ids=true, to_apply=%region_12.13 | all-reduce | flops 5120 | bytes 40960 | tf_op jit(solution)/shard_map/psum | solution.py:175
  433.7 0.6 copy.111
  434.3 3.3 all-to-all-start.2
  437.6 0.6 copy.118
  438.3 4.9 %all-to-all-done.2 = f32[8,24,3]{1,2,0:T(4,128)S(1)} async-done(((f32[8,24,3]{1,2,0:T(4,128)}), f32[8,24,3]{1,2,0:T(4,128)S(1)}, u32[]{:S(2)}, u32[]{:S(2)}) %all-to-all-start.2) | async-done | bytes 2336 | tf_op jit(solution)/shard_map/all_to_all | solution.py:162
  443.3 0.6 gather_fusion.4
  444.0 0.6 copy.117
  (235 shorter events, 8.9 us)
Async XLA Ops:
  7.2 31.1 %all-to-all-start.1 = ((bf16[8,24,6]{1,2,0:T(8,128)(2,1)}), bf16[8,24,6]{1,2,0:T(8,128)(2,1)S(1)}, u32[]{:S(2)}, u32[]{:S(2)}) async-start(bf16[8,24,6]{1,2,0:T(8,128)(2,1)} %select_convert_fusion), calls=%async_computation.1 | async-start | bytes 32768 | tf_op jit(solution)/shard_map/all_to_all | solution.py:135
  38.3 6.1 %copy-start = (f32[10,2,256]{2,1,0:T(2,128)S(1)}, f32[10,2,256]{2,1,0:T(2,128)}, u32[]{:S(2)}) copy-start(f32[10,2,256]{2,1,0:T(2,128)} %param.15) | copy-start | bytes 61444
  38.3 144.3 %all-to-all-start = ((bf16[8,24,128,128]{2,3,1,0:T(8,128)(2,1)}), bf16[8,24,128,128]{2,3,1,0:T(8,128)(2,1)}, u32[]{:S(2)}, u32[]{:S(2)}) async-start(bf16[8,24,128,128]{2,3,1,0:T(8,128)(2,1)} %broadcast_select_fusion), calls=%async_computation | async-start | bytes 12582912 | tf_op jit(solution)/shard_map/all_to_all | solution.py:134
  434.3 8.9 %all-to-all-start.2 = ((f32[8,24,3]{1,2,0:T(4,128)}), f32[8,24,3]{1,2,0:T(4,128)S(1)}, u32[]{:S(2)}, u32[]{:S(2)}) async-start(f32[8,24,3]{1,2,0:T(4,128)} %copy.111), calls=%async_computation.2 | async-start | bytes 32768 | tf_op jit(solution)/shard_map/all_to_all | solution.py:162
where the time goes:
time: 447 us; the launch traced here: 445 us
  other arithmetic  149 us (33%)
  waiting for transfers between devices  141 us (32%)
  local copies, waits for them, and re-layouts  56.4 us (13%)
  matrix products  54.4 us (12%)
  blocking collectives  26.7 us (6%)
  starting transfers between devices  14.9 us (3%)
    all_to_all x1, waiting for transfers between devices, on_device(): lax.all_to_all(patch_buffer, 'dom', split_axis=0, concat_axis=0, tiled=True)  136 us
    reduce_sum x12, other arithmetic, spectral_terms(): jnp.sum(diff_real * diff_real + diff_imag * diff_imag, axis=(1, 2))  131 us
    dot_general x12, matrix products, one_block(): jnp.einsum('bfx,xk->bfk', first_pass, col_table, preferred_element_type=j...  54.1 us
    gather x12, local copies, waits for them, and re-layouts, one_block(): ref_blk = projected_flat[index_blk]  29.9 us
    psum x1, blocking collectives, on_device(): whole_grad = lax.psum(gradient, ('dom', 'rep'))  26.7 us
    gather x2, local copies, waits for them, and re-layouts, on_device(): patches[0][source]  18.8 us
  transfers between devices with their start and end apart: 3, of which 2 were waited for; matrix products, arithmetic and copies ran while one was open for 6% of the time, Pallas kernels for 0%

commit v1 on v0

--- a/solution.py
+++ b/solution.py
@@ -172,7 +172,9 @@
         precision=lax.Precision.HIGHEST,
         preferred_element_type=jnp.float32,
     ).reshape(tilt_dev, 2, node_count)
-    whole_grad = lax.psum(gradient, ("dom", "rep"))
+    whole_grad = gradient
+    for no in ("rep", "dom"):
+        whole_grad = lax.psum(whole_grad, no)
     new_warp = warp_grid - whole_grad / jnp.sqrt(
         whole_grad * whole_grad + TRUST_FLOOR * TRUST_FLOOR
     )

time: 447 us -> 447 us (level)
  no operation moved by 1% of the time
where the time goes in v1:
time: 447 us; the launch traced here: 445 us
  other arithmetic  149 us (33%)
  waiting for transfers between devices  141 us (32%)
  local copies, waits for them, and re-layouts  56.4 us (13%)
  matrix products  54.4 us (12%)
  blocking collectives  26.7 us (6%)
  starting transfers between devices  14.9 us (3%)
    all_to_all x1, waiting for transfers between devices, on_device(): lax.all_to_all(patch_buffer, 'dom', split_axis=0, concat_axis=0, tiled=True)  136 us
    reduce_sum x12, other arithmetic, spectral_terms(): jnp.sum(diff_real * diff_real + diff_imag * diff_imag, axis=(1, 2))  131 us
    dot_general x12, matrix products, one_block(): jnp.einsum('bfx,xk->bfk', first_pass, col_table, preferred_element_type=j...  54.1 us
    gather x12, local copies, waits for them, and re-layouts, one_block(): ref_blk = projected_flat[index_blk]  29.9 us
    psum x1, blocking collectives, on_device(): whole_grad = lax.psum(whole_grad, no)  26.7 us
    gather x2, local copies, waits for them, and re-layouts, on_device(): patches[0][source]  18.8 us
  transfers between devices with their start and end apart: 3, of which 2 were waited for; matrix products, arithmetic and copies ran while one was open for 6% of the time, Pallas kernels for 0%

profile of v1, /device:TPU:0, one launch (start us, length us, event | category | flops | bytes accessed | tf_op | source)
XLA Modules:
  0.0 444.6 jit_solution(1007006649997248516)
XLA Ops:
  0.6 0.7 and_select_fusion.2
  1.7 0.7 fusion.48
  2.4 0.7 multiply_add_fusion.1
  3.3 0.7 bitcast_convert_fusion
  4.1 0.7 convert_bitcast_fusion
  4.7 0.7 stack.8
  5.6 0.8 gather_fusion.2
  6.5 0.6 select_convert_fusion
  7.2 6.4 %all-to-all-start.1 = ((bf16[8,24,6]{1,2,0:T(8,128)(2,1)}), bf16[8,24,6]{1,2,0:T(8,128)(2,1)S(1)}, u32[]{:S(2)}, u32[]{:S(2)}) async-start(bf16[8,24,6]{1,2,0:T(8,128)(2,1)} %select_convert_fusion), calls=%async_computation.1 | async-start | bytes 32768 | tf_op jit(solution)/shard_map/all_to_all | solution.py:135
  13.5 10.2 %gather_fusion.1 = bf16[192,128,128]{2,1,0:T(8,128)(2,1)} fusion(bf16[128,128,128]{2,1,0:T(8,128)(2,1)} %bitcast.181, s32[1024]{0:T(1024)S(1)} %pad_clamp_fusion.3), kind=kCustom, calls=%fused_computation.1 | custom fusion | bytes 12583680 | tf_op jit(solution)/shard_map/gather | solution.py:100
  23.8 8.6 %copy.103 = bf16[8,24,128,128]{2,3,1,0:T(8,128)(2,1)} copy(bf16[8,24,128,128]{3,2,1,0:T(8,128)(2,1)} %bitcast.179) | data formatting | bytes 12582912 | tf_op jit(solution)/shard_map/gather | solution.py:100
  32.4 5.9 %broadcast_select_fusion = bf16[8,24,128,128]{2,3,1,0:T(8,128)(2,1)} fusion(bf16[8,24,128,128]{2,3,1,0:T(8,128)(2,1)} %copy.103, pred[8,24]{1,0:T(8,128)(4,1)S(1)} %broadcast_in_dim.106), kind=kLoop, calls=%fused_computation.65 | loop fusion | flops 3145728 | bytes 12583104 | tf_op jit(solution)/shard_map/jit(_where)/select_n | solution.py:100
  38.3 5.2 %all-to-all-start = ((bf16[8,24,128,128]{2,3,1,0:T(8,128)(2,1)}), bf16[8,24,128,128]{2,3,1,0:T(8,128)(2,1)}, u32[]{:S(2)}, u32[]{:S(2)}) async-start(bf16[8,24,128,128]{2,3,1,0:T(8,128)(2,1)} %broadcast_select_fusion), calls=%async_computation | async-start | bytes 12582912 | tf_op jit(solution)/shard_map/all_to_all | solution.py:134
  44.4 1.1 gather_fusion.3
  46.3 136.3 %all-to-all-done = bf16[8,24,128,128]{2,3,1,0:T(8,128)(2,1)} async-done(((bf16[8,24,128,128]{2,3,1,0:T(8,128)(2,1)}), bf16[8,24,128,128]{2,3,1,0:T(8,128)(2,1)}, u32[]{:S(2)}, u32[]{:S(2)}) %all-to-all-start) | async-done | bytes 6291488 | tf_op jit(solution)/shard_map/all_to_all | solution.py:134
  182.6 223.7 %while.15 = (s32[]{:T(128)}, f32[12,16,3]{1,0,2:T(8,128)S(1)}, bf16[12,16,128,128]{2,3,1,0:T(8,128)(2,1)}, bf16[256,128]{1,0:T(8,128)(2,1)S(1)}, bf16[128,256]{1...) while((s32[]{:T(128)}, f32[12,16,3]{1,0,2:T(8,128)S(1)}, ...), condition=%wide.region_11.12_spmd.clone.clone, body=%wide.region_7.11_spmd.clone.clone.sunk | while | flops 411868064 | bytes 14461309 | solution.py:148
  182.7 4.5 %fusion.62 = f32[16,256,256]{2,1,0:T(8,128)} fusion(bf16[12,16,128,128]{2,3,1,0:T(8,128)(2,1)} %get-tuple-element.403, s32[]{:T(128)} %get-tuple-element.390, bf16[128,256]{1,0:T(8,128)(2,1)S(1)} %get-tuple-element.405, bf16[256,128]{1,0:T(8,128)(2,1)S(1)} %get-tuple-element.404), kind=kOutput, calls=%fused_computation.10.clone.1 | convolution fusion | flops 403177472 | bytes 4850176 | tf_op jit(solution)/shard_map/while/body/eval_jaxpr/bfx,xk->bfk/dot_general | solution.py:129
  187.2 2.5 gather_fusion
  189.8 10.9 %add_reduce_fusion.2 = (f32[16]{0:T(128)S(1)}, f32[16,128,128]{2,1,0:T(8,128)S(1)}) fusion(f32[16,256,256]{2,1,0:T(8,128)} %fusion.62, bf16[16,2,128,128]{3,2,1,0:T(8,128)(2,1)S(1)} %gather_fusion, f32[16,128]{1,0:T(8,128)S(1)} %get-tuple-element.371, f32[16,128]{1,0:T(8,128)S(1)} %get-tuple-element.372, f32[128,128]{1,0:T(8,128)S(1)} %add_multiply_fusion.3, ...), kind=kLoop, calls=%fused_computation.31.clone.1 | loop fusion | flops 7602160 | bytes 6373504 | tf_op jit(solution)/shard_map/while/body/eval_jaxpr/reduce_sum | solution.py:71
  200.8 0.3 multiply_reduce_fusion.4
  201.3 4.5 %fusion.62 = f32[16,256,256]{2,1,0:T(8,128)} fusion(bf16[12,16,128,128]{2,3,1,0:T(8,128)(2,1)} %get-tuple-element.403, s32[]{:T(128)} %get-tuple-element.390, bf16[128,256]{1,0:T(8,128)(2,1)S(1)} %get-tuple-element.405, bf16[256,128]{1,0:T(8,128)(2,1)S(1)} %get-tuple-element.404), kind=kOutput, calls=%fused_computation.10.clone.1 | convolution fusion | flops 403177472 | bytes 4850176 | tf_op jit(solution)/shard_map/while/body/eval_jaxpr/bfx,xk->bfk/dot_general | solution.py:129
  205.9 2.5 gather_fusion
  208.5 10.9 %add_reduce_fusion.2 = (f32[16]{0:T(128)S(1)}, f32[16,128,128]{2,1,0:T(8,128)S(1)}) fusion(f32[16,256,256]{2,1,0:T(8,128)} %fusion.62, bf16[16,2,128,128]{3,2,1,0:T(8,128)(2,1)S(1)} %gather_fusion, f32[16,128]{1,0:T(8,128)S(1)} %get-tuple-element.371, f32[16,128]{1,0:T(8,128)S(1)} %get-tuple-element.372, f32[128,128]{1,0:T(8,128)S(1)} %add_multiply_fusion.3, ...), kind=kLoop, calls=%fused_computation.31.clone.1 | loop fusion | flops 7602160 | bytes 6373504 | tf_op jit(solution)/shard_map/while/body/eval_jaxpr/reduce_sum | solution.py:71
  219.4 0.3 multiply_reduce_fusion.4
  220.0 4.5 %fusion.62 = f32[16,256,256]{2,1,0:T(8,128)} fusion(bf16[12,16,128,128]{2,3,1,0:T(8,128)(2,1)} %get-tuple-element.403, s32[]{:T(128)} %get-tuple-element.390, bf16[128,256]{1,0:T(8,128)(2,1)S(1)} %get-tuple-element.405, bf16[256,128]{1,0:T(8,128)(2,1)S(1)} %get-tuple-element.404), kind=kOutput, calls=%fused_computation.10.clone.1 | convolution fusion | flops 403177472 | bytes 4850176 | tf_op jit(solution)/shard_map/while/body/eval_jaxpr/bfx,xk->bfk/dot_general | solution.py:129
  224.5 2.5 gather_fusion
  227.1 10.9 %add_reduce_fusion.2 = (f32[16]{0:T(128)S(1)}, f32[16,128,128]{2,1,0:T(8,128)S(1)}) fusion(f32[16,256,256]{2,1,0:T(8,128)} %fusion.62, bf16[16,2,128,128]{3,2,1,0:T(8,128)(2,1)S(1)} %gather_fusion, f32[16,128]{1,0:T(8,128)S(1)} %get-tuple-element.371, f32[16,128]{1,0:T(8,128)S(1)} %get-tuple-element.372, f32[128,128]{1,0:T(8,128)S(1)} %add_multiply_fusion.3, ...), kind=kLoop, calls=%fused_computation.31.clone.1 | loop fusion | flops 7602160 | bytes 6373504 | tf_op jit(solution)/shard_map/while/body/eval_jaxpr/reduce_sum | solution.py:71
  238.1 0.3 multiply_reduce_fusion.4
  238.6 4.5 %fusion.62 = f32[16,256,256]{2,1,0:T(8,128)} fusion(bf16[12,16,128,128]{2,3,1,0:T(8,128)(2,1)} %get-tuple-element.403, s32[]{:T(128)} %get-tuple-element.390, bf16[128,256]{1,0:T(8,128)(2,1)S(1)} %get-tuple-element.405, bf16[256,128]{1,0:T(8,128)(2,1)S(1)} %get-tuple-element.404), kind=kOutput, calls=%fused_computation.10.clone.1 | convolution fusion | flops 403177472 | bytes 4850176 | tf_op jit(solution)/shard_map/while/body/eval_jaxpr/bfx,xk->bfk/dot_general | solution.py:129
  243.2 2.5 gather_fusion
  245.8 10.9 %add_reduce_fusion.2 = (f32[16]{0:T(128)S(1)}, f32[16,128,128]{2,1,0:T(8,128)S(1)}) fusion(f32[16,256,256]{2,1,0:T(8,128)} %fusion.62, bf16[16,2,128,128]{3,2,1,0:T(8,128)(2,1)S(1)} %gather_fusion, f32[16,128]{1,0:T(8,128)S(1)} %get-tuple-element.371, f32[16,128]{1,0:T(8,128)S(1)} %get-tuple-element.372, f32[128,128]{1,0:T(8,128)S(1)} %add_multiply_fusion.3, ...), kind=kLoop, calls=%fused_computation.31.clone.1 | loop fusion | flops 7602160 | bytes 6373504 | tf_op jit(solution)/shard_map/while/body/eval_jaxpr/reduce_sum | solution.py:71
  256.7 0.3 multiply_reduce_fusion.4
  257.3 4.5 %fusion.62 = f32[16,256,256]{2,1,0:T(8,128)} fusion(bf16[12,16,128,128]{2,3,1,0:T(8,128)(2,1)} %get-tuple-element.403, s32[]{:T(128)} %get-tuple-element.390, bf16[128,256]{1,0:T(8,128)(2,1)S(1)} %get-tuple-element.405, bf16[256,128]{1,0:T(8,128)(2,1)S(1)} %get-tuple-element.404), kind=kOutput, calls=%fused_computation.10.clone.1 | convolution fusion | flops 403177472 | bytes 4850176 | tf_op jit(solution)/shard_map/while/body/eval_jaxpr/bfx,xk->bfk/dot_general | solution.py:129
  261.8 2.5 gather_fusion
  264.4 10.9 %add_reduce_fusion.2 = (f32[16]{0:T(128)S(1)}, f32[16,128,128]{2,1,0:T(8,128)S(1)}) fusion(f32[16,256,256]{2,1,0:T(8,128)} %fusion.62, bf16[16,2,128,128]{3,2,1,0:T(8,128)(2,1)S(1)} %gather_fusion, f32[16,128]{1,0:T(8,128)S(1)} %get-tuple-element.371, f32[16,128]{1,0:T(8,128)S(1)} %get-tuple-element.372, f32[128,128]{1,0:T(8,128)S(1)} %add_multiply_fusion.3, ...), kind=kLoop, calls=%fused_computation.31.clone.1 | loop fusion | flops 7602160 | bytes 6373504 | tf_op jit(solution)/shard_map/while/body/eval_jaxpr/reduce_sum | solution.py:71
  275.9 4.5 %fusion.62 = f32[16,256,256]{2,1,0:T(8,128)} fusion(bf16[12,16,128,128]{2,3,1,0:T(8,128)(2,1)} %get-tuple-element.403, s32[]{:T(128)} %get-tuple-element.390, bf16[128,256]{1,0:T(8,128)(2,1)S(1)} %get-tuple-element.405, bf16[256,128]{1,0:T(8,128)(2,1)S(1)} %get-tuple-element.404), kind=kOutput, calls=%fused_computation.10.clone.1 | convolution fusion | flops 403177472 | bytes 4850176 | tf_op jit(solution)/shard_map/while/body/eval_jaxpr/bfx,xk->bfk/dot_general | solution.py:129
  280.5 2.5 gather_fusion
  283.1 10.9 %add_reduce_fusion.2 = (f32[16]{0:T(128)S(1)}, f32[16,128,128]{2,1,0:T(8,128)S(1)}) fusion(f32[16,256,256]{2,1,0:T(8,128)} %fusion.62, bf16[16,2,128,128]{3,2,1,0:T(8,128)(2,1)S(1)} %gather_fusion, f32[16,128]{1,0:T(8,128)S(1)} %get-tuple-element.371, f32[16,128]{1,0:T(8,128)S(1)} %get-tuple-element.372, f32[128,128]{1,0:T(8,128)S(1)} %add_multiply_fusion.3, ...), kind=kLoop, calls=%fused_computation.31.clone.1 | loop fusion | flops 7602160 | bytes 6373504 | tf_op jit(solution)/shard_map/while/body/eval_jaxpr/reduce_sum | solution.py:71
  294.6 4.5 %fusion.62 = f32[16,256,256]{2,1,0:T(8,128)} fusion(bf16[12,16,128,128]{2,3,1,0:T(8,128)(2,1)} %get-tuple-element.403, s32[]{:T(128)} %get-tuple-element.390, bf16[128,256]{1,0:T(8,128)(2,1)S(1)} %get-tuple-element.405, bf16[256,128]{1,0:T(8,128)(2,1)S(1)} %get-tuple-element.404), kind=kOutput, calls=%fused_computation.10.clone.1 | convolution fusion | flops 403177472 | bytes 4850176 | tf_op jit(solution)/shard_map/while/body/eval_jaxpr/bfx,xk->bfk/dot_general | solution.py:129
  299.1 2.5 gather_fusion
  301.7 10.9 %add_reduce_fusion.2 = (f32[16]{0:T(128)S(1)}, f32[16,128,128]{2,1,0:T(8,128)S(1)}) fusion(f32[16,256,256]{2,1,0:T(8,128)} %fusion.62, bf16[16,2,128,128]{3,2,1,0:T(8,128)(2,1)S(1)} %gather_fusion, f32[16,128]{1,0:T(8,128)S(1)} %get-tuple-element.371, f32[16,128]{1,0:T(8,128)S(1)} %get-tuple-element.372, f32[128,128]{1,0:T(8,128)S(1)} %add_multiply_fusion.3, ...), kind=kLoop, calls=%fused_computation.31.clone.1 | loop fusion | flops 7602160 | bytes 6373504 | tf_op jit(solution)/shard_map/while/body/eval_jaxpr/reduce_sum | solution.py:71
  313.2 4.5 %fusion.62 = f32[16,256,256]{2,1,0:T(8,128)} fusion(bf16[12,16,128,128]{2,3,1,0:T(8,128)(2,1)} %get-tuple-element.403, s32[]{:T(128)} %get-tuple-element.390, bf16[128,256]{1,0:T(8,128)(2,1)S(1)} %get-tuple-element.405, bf16[256,128]{1,0:T(8,128)(2,1)S(1)} %get-tuple-element.404), kind=kOutput, calls=%fused_computation.10.clone.1 | convolution fusion | flops 403177472 | bytes 4850176 | tf_op jit(solution)/shard_map/while/body/eval_jaxpr/bfx,xk->bfk/dot_general | solution.py:129
  317.8 2.5 gather_fusion
  320.4 10.9 %add_reduce_fusion.2 = (f32[16]{0:T(128)S(1)}, f32[16,128,128]{2,1,0:T(8,128)S(1)}) fusion(f32[16,256,256]{2,1,0:T(8,128)} %fusion.62, bf16[16,2,128,128]{3,2,1,0:T(8,128)(2,1)S(1)} %gather_fusion, f32[16,128]{1,0:T(8,128)S(1)} %get-tuple-element.371, f32[16,128]{1,0:T(8,128)S(1)} %get-tuple-element.372, f32[128,128]{1,0:T(8,128)S(1)} %add_multiply_fusion.3, ...), kind=kLoop, calls=%fused_computation.31.clone.1 | loop fusion | flops 7602160 | bytes 6373504 | tf_op jit(solution)/shard_map/while/body/eval_jaxpr/reduce_sum | solution.py:71
  331.9 4.5 %fusion.62 = f32[16,256,256]{2,1,0:T(8,128)} fusion(bf16[12,16,128,128]{2,3,1,0:T(8,128)(2,1)} %get-tuple-element.403, s32[]{:T(128)} %get-tuple-element.390, bf16[128,256]{1,0:T(8,128)(2,1)S(1)} %get-tuple-element.405, bf16[256,128]{1,0:T(8,128)(2,1)S(1)} %get-tuple-element.404), kind=kOutput, calls=%fused_computation.10.clone.1 | convolution fusion | flops 403177472 | bytes 4850176 | tf_op jit(solution)/shard_map/while/body/eval_jaxpr/bfx,xk->bfk/dot_general | solution.py:129
  336.4 2.5 gather_fusion
  339.0 10.9 %add_reduce_fusion.2 = (f32[16]{0:T(128)S(1)}, f32[16,128,128]{2,1,0:T(8,128)S(1)}) fusion(f32[16,256,256]{2,1,0:T(8,128)} %fusion.62, bf16[16,2,128,128]{3,2,1,0:T(8,128)(2,1)S(1)} %gather_fusion, f32[16,128]{1,0:T(8,128)S(1)} %get-tuple-element.371, f32[16,128]{1,0:T(8,128)S(1)} %get-tuple-element.372, f32[128,128]{1,0:T(8,128)S(1)} %add_multiply_fusion.3, ...), kind=kLoop, calls=%fused_computation.31.clone.1 | loop fusion | flops 7602160 | bytes 6373504 | tf_op jit(solution)/shard_map/while/body/eval_jaxpr/reduce_sum | solution.py:71
  350.5 4.5 %fusion.62 = f32[16,256,256]{2,1,0:T(8,128)} fusion(bf16[12,16,128,128]{2,3,1,0:T(8,128)(2,1)} %get-tuple-element.403, s32[]{:T(128)} %get-tuple-element.390, bf16[128,256]{1,0:T(8,128)(2,1)S(1)} %get-tuple-element.405, bf16[256,128]{1,0:T(8,128)(2,1)S(1)} %get-tuple-element.404), kind=kOutput, calls=%fused_computation.10.clone.1 | convolution fusion | flops 403177472 | bytes 4850176 | tf_op jit(solution)/shard_map/while/body/eval_jaxpr/bfx,xk->bfk/dot_general | solution.py:129
  355.1 2.5 gather_fusion
  357.7 10.9 %add_reduce_fusion.2 = (f32[16]{0:T(128)S(1)}, f32[16,128,128]{2,1,0:T(8,128)S(1)}) fusion(f32[16,256,256]{2,1,0:T(8,128)} %fusion.62, bf16[16,2,128,128]{3,2,1,0:T(8,128)(2,1)S(1)} %gather_fusion, f32[16,128]{1,0:T(8,128)S(1)} %get-tuple-element.371, f32[16,128]{1,0:T(8,128)S(1)} %get-tuple-element.372, f32[128,128]{1,0:T(8,128)S(1)} %add_multiply_fusion.3, ...), kind=kLoop, calls=%fused_computation.31.clone.1 | loop fusion | flops 7602160 | bytes 6373504 | tf_op jit(solution)/shard_map/while/body/eval_jaxpr/reduce_sum | solution.py:71
  369.2 4.5 %fusion.62 = f32[16,256,256]{2,1,0:T(8,128)} fusion(bf16[12,16,128,128]{2,3,1,0:T(8,128)(2,1)} %get-tuple-element.403, s32[]{:T(128)} %get-tuple-element.390, bf16[128,256]{1,0:T(8,128)(2,1)S(1)} %get-tuple-element.405, bf16[256,128]{1,0:T(8,128)(2,1)S(1)} %get-tuple-element.404), kind=kOutput, calls=%fused_computation.10.clone.1 | convolution fusion | flops 403177472 | bytes 4850176 | tf_op jit(solution)/shard_map/while/body/eval_jaxpr/bfx,xk->bfk/dot_general | solution.py:129
  373.7 2.5 gather_fusion
  376.3 10.9 %add_reduce_fusion.2 = (f32[16]{0:T(128)S(1)}, f32[16,128,128]{2,1,0:T(8,128)S(1)}) fusion(f32[16,256,256]{2,1,0:T(8,128)} %fusion.62, bf16[16,2,128,128]{3,2,1,0:T(8,128)(2,1)S(1)} %gather_fusion, f32[16,128]{1,0:T(8,128)S(1)} %get-tuple-element.371, f32[16,128]{1,0:T(8,128)S(1)} %get-tuple-element.372, f32[128,128]{1,0:T(8,128)S(1)} %add_multiply_fusion.3, ...), kind=kLoop, calls=%fused_computation.31.clone.1 | loop fusion | flops 7602160 | bytes 6373504 | tf_op jit(solution)/shard_map/while/body/eval_jaxpr/reduce_sum | solution.py:71
  387.8 4.5 %fusion.62 = f32[16,256,256]{2,1,0:T(8,128)} fusion(bf16[12,16,128,128]{2,3,1,0:T(8,128)(2,1)} %get-tuple-element.403, s32[]{:T(128)} %get-tuple-element.390, bf16[128,256]{1,0:T(8,128)(2,1)S(1)} %get-tuple-element.405, bf16[256,128]{1,0:T(8,128)(2,1)S(1)} %get-tuple-element.404), kind=kOutput, calls=%fused_computation.10.clone.1 | convolution fusion | flops 403177472 | bytes 4850176 | tf_op jit(solution)/shard_map/while/body/eval_jaxpr/bfx,xk->bfk/dot_general | solution.py:129
  392.4 2.5 gather_fusion
  395.0 10.9 %add_reduce_fusion.2 = (f32[16]{0:T(128)S(1)}, f32[16,128,128]{2,1,0:T(8,128)S(1)}) fusion(f32[16,256,256]{2,1,0:T(8,128)} %fusion.62, bf16[16,2,128,128]{3,2,1,0:T(8,128)(2,1)S(1)} %gather_fusion, f32[16,128]{1,0:T(8,128)S(1)} %get-tuple-element.371, f32[16,128]{1,0:T(8,128)S(1)} %get-tuple-element.372, f32[128,128]{1,0:T(8,128)S(1)} %add_multiply_fusion.3, ...), kind=kLoop, calls=%fused_computation.31.clone.1 | loop fusion | flops 7602160 | bytes 6373504 | tf_op jit(solution)/shard_map/while/body/eval_jaxpr/reduce_sum | solution.py:71
  406.6 0.3 fusion.42
  406.9 26.7 %psum.6 = f32[10,2,256]{2,0,1:T(8,128)S(1)} all-reduce(f32[10,2,256]{2,0,1:T(8,128)S(1)} %fusion.42), channel_id=1, replica_groups=mesh['groups'=2,'dom'=8,'tilt'=2,'rep'=1] {'dom'}, use_global_device_ids=true, to_apply=%region_12.13 | all-reduce | flops 5120 | bytes 40960 | tf_op jit(solution)/shard_map/psum | solution.py:177
  433.7 0.6 copy.111
  434.3 3.3 all-to-all-start.2
  437.6 0.6 copy.118
  438.3 4.9 %all-to-all-done.2 = f32[8,24,3]{1,2,0:T(4,128)S(1)} async-done(((f32[8,24,3]{1,2,0:T(4,128)}), f32[8,24,3]{1,2,0:T(4,128)S(1)}, u32[]{:S(2)}, u32[]{:S(2)}) %all-to-all-start.2) | async-done | bytes 2336 | tf_op jit(solution)/shard_map/all_to_all | solution.py:162
  443.3 0.6 gather_fusion.4
  444.0 0.6 copy.117
  (235 shorter events, 8.9 us)
Async XLA Ops:
  7.2 31.1 %all-to-all-start.1 = ((bf16[8,24,6]{1,2,0:T(8,128)(2,1)}), bf16[8,24,6]{1,2,0:T(8,128)(2,1)S(1)}, u32[]{:S(2)}, u32[]{:S(2)}) async-start(bf16[8,24,6]{1,2,0:T(8,128)(2,1)} %select_convert_fusion), calls=%async_computation.1 | async-start | bytes 32768 | tf_op jit(solution)/shard_map/all_to_all | solution.py:135
  38.3 6.1 %copy-start = (f32[10,2,256]{2,1,0:T(2,128)S(1)}, f32[10,2,256]{2,1,0:T(2,128)}, u32[]{:S(2)}) copy-start(f32[10,2,256]{2,1,0:T(2,128)} %param.15) | copy-start | bytes 61444
  38.3 144.3 %all-to-all-start = ((bf16[8,24,128,128]{2,3,1,0:T(8,128)(2,1)}), bf16[8,24,128,128]{2,3,1,0:T(8,128)(2,1)}, u32[]{:S(2)}, u32[]{:S(2)}) async-start(bf16[8,24,128,128]{2,3,1,0:T(8,128)(2,1)} %broadcast_select_fusion), calls=%async_computation | async-start | bytes 12582912 | tf_op jit(solution)/shard_map/all_to_all | solution.py:134
  434.3 8.9 %all-to-all-start.2 = ((f32[8,24,3]{1,2,0:T(4,128)}), f32[8,24,3]{1,2,0:T(4,128)S(1)}, u32[]{:S(2)}, u32[]{:S(2)}) async-start(f32[8,24,3]{1,2,0:T(4,128)} %copy.111), calls=%async_computation.2 | async-start | bytes 32768 | tf_op jit(solution)/shard_map/all_to_all | solution.py:162
